TPU v7x, 32 devices: a whole 2x2x4 slice. The times are simulated.
32 devices in a mesh: group: 2 (over y), seq: 16 (over z, x, core).
Axes of the slice: x: 2, y: 2, z: 4, core: 2. Of those that a mesh axis runs over, the one named last changes fastest.
Arguments:
- query_frames: bfloat16 [16384, 4096], P(('group', 'seq')), parts along dimension 0, may hold values from -5 to 5
- key_frames: bfloat16 [16384, 512], P(('group', 'seq')), parts along dimension 0, may hold values from -5 to 5
- value_frames: bfloat16 [16384, 512], P(('group', 'seq')), parts along dimension 0, may hold values from -6 to 6
- token_counts: int32 [32], P(('group', 'seq')), parts along dimension 0, may hold values from 1 to 511, as said below
- segments: int32 [8192], P('group'), parts along dimension 0, may hold values from 0 to 7, as said below
Outputs:
- attended: bfloat16 [8192, 4096], P(('group', 'seq')), parts along dimension 0
There are 2 independent parts, one for each index of `group`. A program takes and returns all parts, laid end to end along the dimension named above; each array names one. Nothing has to cross between parts.
Inputs may be any that keep to these rules, and one draw needn't show every extreme that they name: `token_counts`: entry d belongs to device d of seq. The counts before entry d sum to a number from d * 256 to d * 256 + 255, and all counts sum to 4096. `segments`: sequence numbers never fall along the positions and each of 0 to 7 appears; each packed sequence covers 1 to 1024 consecutive positions, one exactly 1024; the first covers more than 256.
All inputs are finite; a program needn't handle non-finite values.
Results may differ from a plain program's by a relative error of at most 0.013.
Values may be sent and summed in bfloat16 or wider, within the bound.
A program may use at most 64 MiB of HBM per device.

v0:
```python
import math

import jax
import jax.numpy as jnp
from jax import lax
from jax.sharding import PartitionSpec as P

Q_HEADS = 32
KV_HEADS = 4
HEAD_DIM = 128
SPAN = 256
WINDOW = 5


def passed_along(block, axis, distance):
    devices = range(lax.axis_size(axis))
    route = [(i - distance, i) for i in devices if i - distance in devices]
    return lax.ppermute(block, axis, route)


def attend_block(running, query_rows, key_rows, value_rows, query_part, key_part, segments):
    groups = Q_HEADS // KV_HEADS
    positions = jnp.arange(SPAN, dtype=jnp.int32)
    query_place = query_part * SPAN + positions
    key_place = key_part * SPAN + positions
    query_clip = lax.dynamic_slice_in_dim(segments, query_part * SPAN, SPAN, 0)
    key_clip = lax.dynamic_slice_in_dim(segments, key_part * SPAN, SPAN, 0)
    allowed = (key_place[None, :] <= query_place[:, None]) & (
        key_clip[None, :] == query_clip[:, None]
    )
    highest, totals, summed = running
    scores = jnp.einsum(
        "qhgd,khd->hgqk",
        query_rows.reshape(SPAN, KV_HEADS, groups, HEAD_DIM),
        key_rows.reshape(SPAN, KV_HEADS, HEAD_DIM),
        preferred_element_type=jnp.float32,
    ) * (1.0 / math.sqrt(HEAD_DIM))
    scores = jnp.where(allowed, scores, -jnp.inf)
    new_highest = jnp.maximum(highest, jnp.max(scores, axis=-1))
    factor = jnp.exp(highest - new_highest)
    weights = jnp.exp(scores - new_highest[..., None])
    totals = totals * factor + jnp.sum(weights, axis=-1)
    product = jnp.einsum(
        "hgqk,khd->qhgd",
        weights.astype(jnp.bfloat16),
        value_rows.reshape(SPAN, KV_HEADS, HEAD_DIM),
        preferred_element_type=jnp.float32,
    )
    factor_rows = jnp.transpose(factor, (2, 0, 1))[..., None]
    summed = (summed.reshape(SPAN, KV_HEADS, groups, HEAD_DIM) * factor_rows + product).reshape(
        SPAN, Q_HEADS * HEAD_DIM
    )
    return (new_highest, totals, summed)


def finish(running):
    highest, totals, summed = running
    divisor = jnp.transpose(totals, (2, 0, 1)).reshape(SPAN, Q_HEADS, 1)
    return (
        (summed.reshape(SPAN, Q_HEADS, HEAD_DIM) / divisor)
        .reshape(SPAN, Q_HEADS * HEAD_DIM)
        .astype(jnp.bfloat16)
    )


def shards(query_frames, key_frames, value_frames, token_counts, segments):
    seq_count = lax.axis_size("seq")
    device = lax.axis_index("seq")
    every_count = lax.all_gather(token_counts, "seq", axis=0, tiled=True)
    before = jnp.sum(jnp.where(jnp.arange(seq_count, dtype=jnp.int32) < device, every_count, 0))
    lead_in = before - device * SPAN
    lead_out = lead_in + token_counts[0] - SPAN
    positions = jnp.arange(SPAN, dtype=jnp.int32)[:, None]

    def own_rows(frames):
        padded = jnp.concatenate([jnp.zeros((SPAN, frames.shape[1]), frames.dtype), frames], axis=0)
        return lax.dynamic_slice_in_dim(padded, SPAN - lead_in, SPAN, 0)

    def tail_rows(frames):
        sliced = lax.dynamic_slice_in_dim(frames, SPAN - lead_in, SPAN, 0)
        return jnp.where(positions < lead_out, sliced, jnp.zeros_like(sliced))

    arrived = passed_along(
        (tail_rows(query_frames), tail_rows(key_frames), tail_rows(value_frames)), "seq", 1
    )
    early = positions < lead_in
    queries = jnp.where(early, arrived[0], own_rows(query_frames))
    key_rows = jnp.where(early, arrived[1], own_rows(key_frames))
    value_rows = jnp.where(early, arrived[2], own_rows(value_frames))
    groups = Q_HEADS // KV_HEADS
    initial = (
        jnp.full((KV_HEADS, groups, SPAN), -1e30, jnp.float32),
        jnp.zeros((KV_HEADS, groups, SPAN), jnp.float32),
        jnp.zeros((SPAN, Q_HEADS * HEAD_DIM), jnp.float32),
    )
    running = attend_block(initial, queries, key_rows, value_rows, device, device, segments)

    def visit(turn_number, carried):
        moving, current = carried
        moving = passed_along((moving[0], moving[1]), "seq", 1)
        block_number = (device - turn_number) % seq_count
        return (
            moving,
            attend_block(current, queries, moving[0], moving[1], device, block_number, segments),
        )

    carried = lax.fori_loop(1, WINDOW, visit, ((key_rows, value_rows), running))
    return finish(carried[1])


def solution(mesh):
    in_specs = (
        P(("group", "seq"), None),
        P(("group", "seq"), None),
        P(("group", "seq"), None),
        P(("group", "seq")),
        P("group"),
    )
    out_specs = P(("group", "seq"), None)
    return jax.shard_map(shards, mesh=mesh, in_specs=in_specs, out_specs=out_specs, check_vma=False)
```

profile of v0, /device:TPU:0, one launch (start us, length us, event | category | flops | bytes accessed | tf_op | source)
XLA Modules:
  0.0 149.2 jit_solution(12138810646776412305)
XLA Ops:
  2.7 13.7 %all-reduce.3 = s32[16]{0:T(128)S(1)} all-reduce(s32[16]{0:T(128)S(1)} %dynamic-update-slice), channel_id=1, replica_groups=mesh['group'=2,'seq'=16] {'seq'}, use_global_device_ids=true, to_apply=%add.3 | all-reduce | flops 16 | bytes 128
  17.7 2.3 %dynamic-slice_select_fusion = bf16[256,4096]{1,0:T(8,128)(2,1)S(1)} fusion(bf16[512,4096]{1,0:T(8,128)(2,1)} %param.7, s32[]{:T(128)S(6)} %select_n.90, pred[256]{0:T(512)(128)(4,1)S(1)} %iota_compare_fusion), kind=kLoop, calls=%fused_computation.38 | loop fusion | flops 1048576 | bytes 4194564 | tf_op jit(solution)/shard_map/jit(_where)/select_n | solution.py:81
  20.1 2.6 %collective-permute-start.4 = (bf16[256,4096]{1,0:T(8,128)(2,1)S(1)}, bf16[256,4096]{1,0:T(8,128)(2,1)}, u32[]{:S(2)}, u32[]{:S(2)}) collective-permute-start(bf16[256,4096]{1,0:T(8,128)(2,1)S(1)} %dynamic-slice_select_fusion), channel_id=1, source_target_pairs={{0,1},{1,2},{2,3},{3,4},{4,5},{5,6},{6,7},{7,8},{8,9},{9,10},{10,1... | collective-permute-start | bytes 6291464 | tf_op jit(solution)/shard_map/ppermute | solution.py:18
  25.1 2.9 %collective-permute-start.2 = (bf16[256,512]{0,1:T(8,128)(2,1)}, bf16[256,512]{0,1:T(8,128)(2,1)}, u32[]{:S(2)}, u32[]{:S(2)}) collective-permute-start(bf16[256,512]{0,1:T(8,128)(2,1)} %get-tuple-element.288), channel_id=1, source_target_pairs={{0,1},{1,2},{2,3},{3,4},{4,5},{5,6},{6,7},{7,8},{8,9},{9,10},{10,1... | collective-permute-start | bytes 786440 | tf_op jit(solution)/shard_map/ppermute | solution.py:18
  32.3 3.7 %fusion.26 = bf16[256,4096]{1,0:T(8,128)(2,1)S(1)} fusion(bf16[256,4096]{1,0:T(8,128)(2,1)} %collective-permute-done.4, s32[]{:T(128)S(6)} %select_n.92, bf16[512,4096]{1,0:T(8,128)(2,1)} %param.7, pred[256]{0:T(512)(128)(4,1)S(1)} %iota_compare_fusion.1), kind=kLoop, calls=%fused_computation.35 | loop fusion | flops 1048576 | bytes 8388868 | tf_op jit(solution)/shard_map/jit(_where)/select_n | solution.py:87
  36.5 2.3 %fusion.18 = (f32[4,8,256]{2,1,0:T(8,128)S(1)}, f32[4,256,256,8]{2,1,3,0:T(8,128)S(1)}) fusion(pred[256,256]{0,1:T(8,128)(4,1)S(1)} %compare_and_fusion.1, bf16[256,4,128,1]{0,2,3,1:T(8,128)(2,1)S(1)} %bitcast.112, bf16[256,4,8,128]{3,2,1,0:T(8,128)(2,1)S(1)} %bitcast.109), kind=kOutput, calls=%fused_computation.25 | convolution fusion | flops 543154176 | bytes 10846208 | tf_op jit(solution)/shard_map/qhgd,khd->hgqk/dot_general | solution.py:32
  40.6 4.3 %bitcast_add_fusion.1 = f32[256,4,8,128]{0,3,2,1:T(8,128)} fusion(f32[256,4,8]{0,2,1:T(8,128)S(1)} %get-tuple-element.283, bf16[256,4,128,1]{0,2,3,1:T(8,128)(2,1)S(1)} %bitcast.111, f32[4,256,256,8]{2,1,3,0:T(8,128)S(1)} %get-tuple-element.290, f32[4,8,256]{2,1,0:T(8,128)S(1)} %broadcast_maximum_fusion, pred[256,256]{0,1:T(8,128)(4,1)S(1)} %compare_and_fusion.1), kind=kOutput, calls=%fused_computation.30 | convolution fusion | flops 546308096 | bytes 12976128 | tf_op jit(solution)/shard_map/hgqk,khd->qhgd/dot_general | solution.py:43
  44.9 92.3 %while.23 = (s32[]{:T(128)}, bf16[256,512]{0,1:T(8,128)(2,1)S(1)}, bf16[256,512]{0,1:T(8,128)(2,1)S(1)}, f32[4,8,256]{2,1,0:T(8,128)S(1)}, f32[4,8,256]{2,1,0:T(...) while((s32[]{:T(128)}, bf16[256,512]{0,1:T(8,128)(2,1)S(1)}, ...), condition=%wide.region_6.7_spmd, body=%wide.region_3.6_spmd.sunk | while | flops 1099129344 | bytes 94642712 | solution.py:107
  44.9 22.4 %collective-permute-start = (bf16[256,512]{0,1:T(8,128)(2,1)S(1)}, bf16[256,512]{0,1:T(8,128)(2,1)S(1)}, u32[]{:S(2)}, u32[]{:S(2)}) collective-permute-start(bf16[256,512]{0,1:T(8,128)(2,1)S(1)} %get-tuple-element.388), channel_id=1, source_target_pairs={{0,1},{1,2},{2,3},{3,4},{4,5},{5,6},{6,7},{7,8},{8,9},{9,10},{10,1... | collective-permute-start | bytes 786440 | tf_op jit(solution)/shard_map/while/body/eval_jaxpr/ppermute | solution.py:18
  67.3 4.1 %collective-permute-start.1 = (bf16[256,512]{0,1:T(8,128)(2,1)S(1)}, bf16[256,512]{0,1:T(8,128)(2,1)S(1)}, u32[]{:S(2)}, u32[]{:S(2)}) collective-permute-start(bf16[256,512]{0,1:T(8,128)(2,1)S(1)} %get-tuple-element.389), channel_id=1, source_target_pairs={{0,1},{1,2},{2,3},{3,4},{4,5},{5,6},{6,7},{7,8},{8,9},{9,10},{10,1... | collective-permute-start | bytes 786440 | tf_op jit(solution)/shard_map/while/body/eval_jaxpr/ppermute | solution.py:18
  71.4 2.1 %copy.55 = bf16[32,8,32,128]{3,2,1,0:T(8,128)(2,1)S(1)} copy(bf16[32,8,32,128]{3,1,2,0:T(8,128)(2,1)} %bitcast.105) | data formatting | bytes 4194304 | tf_op jit(solution)/shard_map/while
  74.4 2.3 %fusion.51 = (f32[4,8,256]{2,1,0:T(8,128)S(1)}, f32[4,256,256,8]{2,1,3,0:T(8,128)S(1)}) fusion(pred[256,256]{0,1:T(8,128)(4,1)S(1)} %compare_and_fusion.3, bf16[256,4,128,1]{0,2,3,1:T(8,128)(2,1)S(1)} %bitcast.107, bf16[256,4,8,128]{3,2,1,0:T(8,128)(2,1)S(1)} %bitcast.100), kind=kOutput, calls=%fused_computation.4.clone.1 | convolution fusion | flops 543154176 | bytes 10846208 | tf_op jit(solution)/shard_map/while/body/eval_jaxpr/qhgd,khd->hgqk/dot_general | solution.py:32
  78.9 2.7 %bitcast_add_fusion.3 = f32[256,4,8,128]{0,3,2,1:T(8,128)S(1)} fusion(f32[256,4,8,128]{0,3,2,1:T(8,128)S(1)} %bitcast.102, f32[256,4,8]{0,2,1:T(8,128)S(1)} %get-tuple-element.369, bf16[256,4,128,1]{0,2,3,1:T(8,128)(2,1)S(1)} %bitcast.106, f32[4,256,256,8]{2,1,3,0:T(8,128)S(1)} %get-tuple-element.368, f32[4,8,256]{2,1,0:T(8,128)S(1)} %get-tuple-element.407, ...), kind=kOutput, calls=%fused_computation.6.clone.1 | convolution fusion | flops 547356672 | bytes 17170432 | tf_op jit(solution)/shard_map/while/body/eval_jaxpr/hgqk,khd->qhgd/dot_general | solution.py:43
  85.5 3.9 %collective-permute-start.1 = (bf16[256,512]{0,1:T(8,128)(2,1)S(1)}, bf16[256,512]{0,1:T(8,128)(2,1)S(1)}, u32[]{:S(2)}, u32[]{:S(2)}) collective-permute-start(bf16[256,512]{0,1:T(8,128)(2,1)S(1)} %get-tuple-element.389), channel_id=1, source_target_pairs={{0,1},{1,2},{2,3},{3,4},{4,5},{5,6},{6,7},{7,8},{8,9},{9,10},{10,1... | collective-permute-start | bytes 786440 | tf_op jit(solution)/shard_map/while/body/eval_jaxpr/ppermute | solution.py:18
  92.5 2.3 %fusion.51 = (f32[4,8,256]{2,1,0:T(8,128)S(1)}, f32[4,256,256,8]{2,1,3,0:T(8,128)S(1)}) fusion(pred[256,256]{0,1:T(8,128)(4,1)S(1)} %compare_and_fusion.3, bf16[256,4,128,1]{0,2,3,1:T(8,128)(2,1)S(1)} %bitcast.107, bf16[256,4,8,128]{3,2,1,0:T(8,128)(2,1)S(1)} %bitcast.100), kind=kOutput, calls=%fused_computation.4.clone.1 | convolution fusion | flops 543154176 | bytes 10846208 | tf_op jit(solution)/shard_map/while/body/eval_jaxpr/qhgd,khd->hgqk/dot_general | solution.py:32
  97.0 2.7 %bitcast_add_fusion.3 = f32[256,4,8,128]{0,3,2,1:T(8,128)S(1)} fusion(f32[256,4,8,128]{0,3,2,1:T(8,128)S(1)} %bitcast.102, f32[256,4,8]{0,2,1:T(8,128)S(1)} %get-tuple-element.369, bf16[256,4,128,1]{0,2,3,1:T(8,128)(2,1)S(1)} %bitcast.106, f32[4,256,256,8]{2,1,3,0:T(8,128)S(1)} %get-tuple-element.368, f32[4,8,256]{2,1,0:T(8,128)S(1)} %get-tuple-element.407, ...), kind=kOutput, calls=%fused_computation.6.clone.1 | convolution fusion | flops 547356672 | bytes 17170432 | tf_op jit(solution)/shard_map/while/body/eval_jaxpr/hgqk,khd->qhgd/dot_general | solution.py:43
  103.6 3.6 %collective-permute-start.1 = (bf16[256,512]{0,1:T(8,128)(2,1)S(1)}, bf16[256,512]{0,1:T(8,128)(2,1)S(1)}, u32[]{:S(2)}, u32[]{:S(2)}) collective-permute-start(bf16[256,512]{0,1:T(8,128)(2,1)S(1)} %get-tuple-element.389), channel_id=1, source_target_pairs={{0,1},{1,2},{2,3},{3,4},{4,5},{5,6},{6,7},{7,8},{8,9},{9,10},{10,1... | collective-permute-start | bytes 786440 | tf_op jit(solution)/shard_map/while/body/eval_jaxpr/ppermute | solution.py:18
  110.3 2.3 %fusion.51 = (f32[4,8,256]{2,1,0:T(8,128)S(1)}, f32[4,256,256,8]{2,1,3,0:T(8,128)S(1)}) fusion(pred[256,256]{0,1:T(8,128)(4,1)S(1)} %compare_and_fusion.3, bf16[256,4,128,1]{0,2,3,1:T(8,128)(2,1)S(1)} %bitcast.107, bf16[256,4,8,128]{3,2,1,0:T(8,128)(2,1)S(1)} %bitcast.100), kind=kOutput, calls=%fused_computation.4.clone.1 | convolution fusion | flops 543154176 | bytes 10846208 | tf_op jit(solution)/shard_map/while/body/eval_jaxpr/qhgd,khd->hgqk/dot_general | solution.py:32
  114.8 2.7 %bitcast_add_fusion.3 = f32[256,4,8,128]{0,3,2,1:T(8,128)S(1)} fusion(f32[256,4,8,128]{0,3,2,1:T(8,128)S(1)} %bitcast.102, f32[256,4,8]{0,2,1:T(8,128)S(1)} %get-tuple-element.369, bf16[256,4,128,1]{0,2,3,1:T(8,128)(2,1)S(1)} %bitcast.106, f32[4,256,256,8]{2,1,3,0:T(8,128)S(1)} %get-tuple-element.368, f32[4,8,256]{2,1,0:T(8,128)S(1)} %get-tuple-element.407, ...), kind=kOutput, calls=%fused_computation.6.clone.1 | convolution fusion | flops 547356672 | bytes 17170432 | tf_op jit(solution)/shard_map/while/body/eval_jaxpr/hgqk,khd->qhgd/dot_general | solution.py:43
  121.4 3.6 %collective-permute-start.1 = (bf16[256,512]{0,1:T(8,128)(2,1)S(1)}, bf16[256,512]{0,1:T(8,128)(2,1)S(1)}, u32[]{:S(2)}, u32[]{:S(2)}) collective-permute-start(bf16[256,512]{0,1:T(8,128)(2,1)S(1)} %get-tuple-element.389), channel_id=1, source_target_pairs={{0,1},{1,2},{2,3},{3,4},{4,5},{5,6},{6,7},{7,8},{8,9},{9,10},{10,1... | collective-permute-start | bytes 786440 | tf_op jit(solution)/shard_map/while/body/eval_jaxpr/ppermute | solution.py:18
  128.0 2.3 %fusion.51 = (f32[4,8,256]{2,1,0:T(8,128)S(1)}, f32[4,256,256,8]{2,1,3,0:T(8,128)S(1)}) fusion(pred[256,256]{0,1:T(8,128)(4,1)S(1)} %compare_and_fusion.3, bf16[256,4,128,1]{0,2,3,1:T(8,128)(2,1)S(1)} %bitcast.107, bf16[256,4,8,128]{3,2,1,0:T(8,128)(2,1)S(1)} %bitcast.100), kind=kOutput, calls=%fused_computation.4.clone.1 | convolution fusion | flops 543154176 | bytes 10846208 | tf_op jit(solution)/shard_map/while/body/eval_jaxpr/qhgd,khd->hgqk/dot_general | solution.py:32
  132.6 2.7 %bitcast_add_fusion.3 = f32[256,4,8,128]{0,3,2,1:T(8,128)S(1)} fusion(f32[256,4,8,128]{0,3,2,1:T(8,128)S(1)} %bitcast.102, f32[256,4,8]{0,2,1:T(8,128)S(1)} %get-tuple-element.369, bf16[256,4,128,1]{0,2,3,1:T(8,128)(2,1)S(1)} %bitcast.106, f32[4,256,256,8]{2,1,3,0:T(8,128)S(1)} %get-tuple-element.368, f32[4,8,256]{2,1,0:T(8,128)S(1)} %get-tuple-element.407, ...), kind=kOutput, calls=%fused_computation.6.clone.1 | convolution fusion | flops 547356672 | bytes 17170432 | tf_op jit(solution)/shard_map/while/body/eval_jaxpr/hgqk,khd->qhgd/dot_general | solution.py:43
  137.3 5.7 %copy.29 = f32[256,4096]{1,0:T(8,128)} copy(f32[256,4096]{0,1:T(8,128)} %get-tuple-element.242) | data formatting | bytes 8388608 | tf_op jit(solution)/shard_map/while | solution.py:107
  145.2 4.0 %fusion.21 = bf16[256,4096]{1,0:T(8,128)(2,1)} fusion(f32[256,4096]{1,0:T(8,128)S(1)} %copy-done.4, f32[32,8,32,128]{3,2,1,0:T(8,128)S(1)} %bitcast.108), kind=kLoop, calls=%fused_computation.29 | loop fusion | flops 2097152 | bytes 10485760 | tf_op jit(solution)/shard_map/convert_element_type | solution.py:62
  (113 shorter events, 45.8 us)
Async XLA Ops:
  0.0 22.7 %copy-start.7 = (bf16[512,512]{1,0:T(8,128)(2,1)S(1)}, bf16[512,512]{1,0:T(8,128)(2,1)}, u32[]{:S(2)}) copy-start(bf16[512,512]{1,0:T(8,128)(2,1)} %param.8) | copy-start | bytes 1572868
  20.1 12.2 %collective-permute-start.4 = (bf16[256,4096]{1,0:T(8,128)(2,1)S(1)}, bf16[256,4096]{1,0:T(8,128)(2,1)}, u32[]{:S(2)}, u32[]{:S(2)}) collective-permute-start(bf16[256,4096]{1,0:T(8,128)(2,1)S(1)} %dynamic-slice_select_fusion), channel_id=1, source_target_pairs={{0,1},{1,2},{2,3},{3,4},{4,5},{5,6},{6,7},{7,8},{8,9},{9,10},{10,1... | collective-permute-start | bytes 6291464 | tf_op jit(solution)/shard_map/ppermute | solution.py:18
  25.1 5.8 %collective-permute-start.2 = (bf16[256,512]{0,1:T(8,128)(2,1)}, bf16[256,512]{0,1:T(8,128)(2,1)}, u32[]{:S(2)}, u32[]{:S(2)}) collective-permute-start(bf16[256,512]{0,1:T(8,128)(2,1)} %get-tuple-element.288), channel_id=1, source_target_pairs={{0,1},{1,2},{2,3},{3,4},{4,5},{5,6},{6,7},{7,8},{8,9},{9,10},{10,1... | collective-permute-start | bytes 786440 | tf_op jit(solution)/shard_map/ppermute | solution.py:18
  28.0 2.9 %collective-permute-start.3 = (bf16[256,512]{0,1:T(8,128)(2,1)S(1)}, bf16[256,512]{0,1:T(8,128)(2,1)}, u32[]{:S(2)}, u32[]{:S(2)}) collective-permute-start(bf16[256,512]{0,1:T(8,128)(2,1)S(1)} %get-tuple-element.287), channel_id=1, source_target_pairs={{0,1},{1,2},{2,3},{3,4},{4,5},{5,6},{6,7},{7,8},{8,9},{9,10},{10,1... | collective-permute-start | bytes 786440 | tf_op jit(solution)/shard_map/ppermute | solution.py:18
  32.3 4.2 %copy-start.5 = (bf16[256,512]{0,1:T(8,128)(2,1)}, bf16[256,512]{0,1:T(8,128)(2,1)S(1)}, u32[]{:S(2)}) copy-start(bf16[256,512]{0,1:T(8,128)(2,1)S(1)} %get-tuple-element.371) | copy-start | bytes 786436
  40.6 4.3 %copy-start.6 = (bf16[256,512]{0,1:T(8,128)(2,1)S(1)}, bf16[256,512]{0,1:T(8,128)(2,1)}, u32[]{:S(2)}) copy-start(bf16[256,512]{0,1:T(8,128)(2,1)} %copy-done.5) | copy-start | bytes 786436
  44.9 26.5 %copy-start.2 = (bf16[256,4096]{1,0:T(8,128)(2,1)}, bf16[256,4096]{1,0:T(8,128)(2,1)S(1)}, u32[]{:S(2)}) copy-start(bf16[256,4096]{1,0:T(8,128)(2,1)S(1)} %get-tuple-element.414) | copy-start | bytes 6291460 | tf_op jit(solution)/shard_map/while
  44.9 29.5 %collective-permute-start = (bf16[256,512]{0,1:T(8,128)(2,1)S(1)}, bf16[256,512]{0,1:T(8,128)(2,1)S(1)}, u32[]{:S(2)}, u32[]{:S(2)}) collective-permute-start(bf16[256,512]{0,1:T(8,128)(2,1)S(1)} %get-tuple-element.388), channel_id=1, source_target_pairs={{0,1},{1,2},{2,3},{3,4},{4,5},{5,6},{6,7},{7,8},{8,9},{9,10},{10,1... | collective-permute-start | bytes 786440 | tf_op jit(solution)/shard_map/while/body/eval_jaxpr/ppermute | solution.py:18
  67.3 11.3 %collective-permute-start.1 = (bf16[256,512]{0,1:T(8,128)(2,1)S(1)}, bf16[256,512]{0,1:T(8,128)(2,1)S(1)}, u32[]{:S(2)}, u32[]{:S(2)}) collective-permute-start(bf16[256,512]{0,1:T(8,128)(2,1)S(1)} %get-tuple-element.389), channel_id=1, source_target_pairs={{0,1},{1,2},{2,3},{3,4},{4,5},{5,6},{6,7},{7,8},{8,9},{9,10},{10,1... | collective-permute-start | bytes 786440 | tf_op jit(solution)/shard_map/while/body/eval_jaxpr/ppermute | solution.py:18
  78.9 4.7 %copy-start.3 = (bf16[256,4096]{1,0:T(8,128)(2,1)S(1)}, bf16[256,4096]{1,0:T(8,128)(2,1)}, u32[]{:S(2)}) copy-start(bf16[256,4096]{1,0:T(8,128)(2,1)} %copy-done.2) | copy-start | bytes 6291460 | tf_op jit(solution)/shard_map/while
  83.6 5.9 %copy-start.2 = (bf16[256,4096]{1,0:T(8,128)(2,1)}, bf16[256,4096]{1,0:T(8,128)(2,1)S(1)}, u32[]{:S(2)}) copy-start(bf16[256,4096]{1,0:T(8,128)(2,1)S(1)} %get-tuple-element.414) | copy-start | bytes 6291460 | tf_op jit(solution)/shard_map/while
  83.6 8.9 %collective-permute-start = (bf16[256,512]{0,1:T(8,128)(2,1)S(1)}, bf16[256,512]{0,1:T(8,128)(2,1)S(1)}, u32[]{:S(2)}, u32[]{:S(2)}) collective-permute-start(bf16[256,512]{0,1:T(8,128)(2,1)S(1)} %get-tuple-element.388), channel_id=1, source_target_pairs={{0,1},{1,2},{2,3},{3,4},{4,5},{5,6},{6,7},{7,8},{8,9},{9,10},{10,1... | collective-permute-start | bytes 786440 | tf_op jit(solution)/shard_map/while/body/eval_jaxpr/ppermute | solution.py:18
  85.5 11.2 %collective-permute-start.1 = (bf16[256,512]{0,1:T(8,128)(2,1)S(1)}, bf16[256,512]{0,1:T(8,128)(2,1)S(1)}, u32[]{:S(2)}, u32[]{:S(2)}) collective-permute-start(bf16[256,512]{0,1:T(8,128)(2,1)S(1)} %get-tuple-element.389), channel_id=1, source_target_pairs={{0,1},{1,2},{2,3},{3,4},{4,5},{5,6},{6,7},{7,8},{8,9},{9,10},{10,1... | collective-permute-start | bytes 786440 | tf_op jit(solution)/shard_map/while/body/eval_jaxpr/ppermute | solution.py:18
  94.8 2.2 %copy-start = (f32[256,4096]{0,1:T(8,128)S(1)}, f32[256,4096]{0,1:T(8,128)}, u32[]{:S(2)}) copy-start(f32[256,4096]{0,1:T(8,128)} %get-tuple-element.392) | copy-start | bytes 12582916 | tf_op jit(solution)/shard_map/while
  97.0 4.7 %copy-start.3 = (bf16[256,4096]{1,0:T(8,128)(2,1)S(1)}, bf16[256,4096]{1,0:T(8,128)(2,1)}, u32[]{:S(2)}) copy-start(bf16[256,4096]{1,0:T(8,128)(2,1)} %copy-done.2) | copy-start | bytes 6291460 | tf_op jit(solution)/shard_map/while
  101.7 5.6 %copy-start.2 = (bf16[256,4096]{1,0:T(8,128)(2,1)}, bf16[256,4096]{1,0:T(8,128)(2,1)S(1)}, u32[]{:S(2)}) copy-start(bf16[256,4096]{1,0:T(8,128)(2,1)S(1)} %get-tuple-element.414) | copy-start | bytes 6291460 | tf_op jit(solution)/shard_map/while
  101.7 8.6 %collective-permute-start = (bf16[256,512]{0,1:T(8,128)(2,1)S(1)}, bf16[256,512]{0,1:T(8,128)(2,1)S(1)}, u32[]{:S(2)}, u32[]{:S(2)}) collective-permute-start(bf16[256,512]{0,1:T(8,128)(2,1)S(1)} %get-tuple-element.388), channel_id=1, source_target_pairs={{0,1},{1,2},{2,3},{3,4},{4,5},{5,6},{6,7},{7,8},{8,9},{9,10},{10,1... | collective-permute-start | bytes 786440 | tf_op jit(solution)/shard_map/while/body/eval_jaxpr/ppermute | solution.py:18
  103.6 10.8 %collective-permute-start.1 = (bf16[256,512]{0,1:T(8,128)(2,1)S(1)}, bf16[256,512]{0,1:T(8,128)(2,1)S(1)}, u32[]{:S(2)}, u32[]{:S(2)}) collective-permute-start(bf16[256,512]{0,1:T(8,128)(2,1)S(1)} %get-tuple-element.389), channel_id=1, source_target_pairs={{0,1},{1,2},{2,3},{3,4},{4,5},{5,6},{6,7},{7,8},{8,9},{9,10},{10,1... | collective-permute-start | bytes 786440 | tf_op jit(solution)/shard_map/while/body/eval_jaxpr/ppermute | solution.py:18
  114.8 4.7 %copy-start.3 = (bf16[256,4096]{1,0:T(8,128)(2,1)S(1)}, bf16[256,4096]{1,0:T(8,128)(2,1)}, u32[]{:S(2)}) copy-start(bf16[256,4096]{1,0:T(8,128)(2,1)} %copy-done.2) | copy-start | bytes 6291460 | tf_op jit(solution)/shard_map/while
  119.5 5.6 %copy-start.2 = (bf16[256,4096]{1,0:T(8,128)(2,1)}, bf16[256,4096]{1,0:T(8,128)(2,1)S(1)}, u32[]{:S(2)}) copy-start(bf16[256,4096]{1,0:T(8,128)(2,1)S(1)} %get-tuple-element.414) | copy-start | bytes 6291460 | tf_op jit(solution)/shard_map/while
  119.5 8.6 %collective-permute-start = (bf16[256,512]{0,1:T(8,128)(2,1)S(1)}, bf16[256,512]{0,1:T(8,128)(2,1)S(1)}, u32[]{:S(2)}, u32[]{:S(2)}) collective-permute-start(bf16[256,512]{0,1:T(8,128)(2,1)S(1)} %get-tuple-element.388), channel_id=1, source_target_pairs={{0,1},{1,2},{2,3},{3,4},{4,5},{5,6},{6,7},{7,8},{8,9},{9,10},{10,1... | collective-permute-start | bytes 786440 | tf_op jit(solution)/shard_map/while/body/eval_jaxpr/ppermute | solution.py:18
  121.4 10.8 %collective-permute-start.1 = (bf16[256,512]{0,1:T(8,128)(2,1)S(1)}, bf16[256,512]{0,1:T(8,128)(2,1)S(1)}, u32[]{:S(2)}, u32[]{:S(2)}) collective-permute-start(bf16[256,512]{0,1:T(8,128)(2,1)S(1)} %get-tuple-element.389), channel_id=1, source_target_pairs={{0,1},{1,2},{2,3},{3,4},{4,5},{5,6},{6,7},{7,8},{8,9},{9,10},{10,1... | collective-permute-start | bytes 786440 | tf_op jit(solution)/shard_map/while/body/eval_jaxpr/ppermute | solution.py:18
  130.4 2.2 %copy-start = (f32[256,4096]{0,1:T(8,128)S(1)}, f32[256,4096]{0,1:T(8,128)}, u32[]{:S(2)}) copy-start(f32[256,4096]{0,1:T(8,128)} %get-tuple-element.392) | copy-start | bytes 12582916 | tf_op jit(solution)/shard_map/while
  132.6 4.7 %copy-start.3 = (bf16[256,4096]{1,0:T(8,128)(2,1)S(1)}, bf16[256,4096]{1,0:T(8,128)(2,1)}, u32[]{:S(2)}) copy-start(bf16[256,4096]{1,0:T(8,128)(2,1)} %copy-done.2) | copy-start | bytes 6291460 | tf_op jit(solution)/shard_map/while
  (7 other events, 14.3 us)
where the time goes:
time: 150 us; the launch traced here: 149 us
  starting transfers between devices  50.8 us (34%)
  local copies, waits for them, and re-layouts  33 us (22%)
  matrix products  26.7 us (18%)
  other arithmetic  22.8 us (15%)
  blocking collectives  13.7 us (9%)
    ppermute x11, starting transfers between devices, passed_along(): return lax.ppermute(block, axis, route)  50.8 us
    while x48, local copies, waits for them, and re-layouts  17.3 us
    dot_general x5, matrix products, attend_block(): jnp.einsum('hgqk,khd->qhgd', weights.astype(jnp.bfloat16), value_rows.res...  15.1 us
    unnamed x1, blocking collectives  13.7 us
    dot_general x5, matrix products, attend_block(): jnp.einsum('qhgd,khd->hgqk', query_rows.reshape(SPAN, KV_HEADS, groups, H...  11.5 us
    reduce_sum x5, other arithmetic, attend_block(): totals = totals * factor + jnp.sum(weights, axis=-1)  8.95 us
    while x1, local copies, waits for them, and re-layouts, shards(): carried = lax.fori_loop(1, WINDOW, visit, ((key_rows, value_rows), running))  5.65 us
    unnamed x14, local copies, waits for them, and re-layouts  5 us
  transfers between devices with their start and end apart: 11, of which 0 were waited for; matrix products, arithmetic and copies ran while one was open for 22% of the time, Pallas kernels for 0%

commit v1 on v0

v1 whole, which is shorter than its diff:
```python
import functools
import math

import jax
import jax.numpy as jnp
from jax import lax
from jax.experimental import pallas as pl
from jax.experimental.pallas import tpu as pltpu
from jax.sharding import PartitionSpec as P

Q_HEADS = 32
KV_HEADS = 4
HEAD_DIM = 128
SPAN = 256
WINDOW = 5
CHUNK_HEADS = 4
CHUNK = CHUNK_HEADS * HEAD_DIM
CHUNKS = Q_HEADS // CHUNK_HEADS
EARLY = 2
KW = KV_HEADS * HEAD_DIM
LAST = WINDOW - 1
LOW = -(2.0**100)
BF16 = jnp.bfloat16
F32 = jnp.float32


def one_hot(rows, columns, shift):
    row = lax.broadcasted_iota(jnp.int32, (rows, columns), 0)
    column = lax.broadcasted_iota(jnp.int32, (rows, columns), 1)
    return jnp.where(column == row + shift, 1.0, 0.0).astype(BF16)


def kernel(
    n, count_ref, seg_ref, qf, kf, vf, out,
    counts, q_in, q_tail, q_got, kv_in, kv_tail, kv_got, window, keys_t, vals, causal, clips, o_buf,
    in_sem, kv_in_sem, out_sem, cnt_send, cnt_recv, tail_send, tail_recv, q_send, q_recv, kv_send, kv_recv,
):
    me = lax.axis_index("seq")
    core = lax.rem(me, 2)
    cap = kv_in.shape[0]

    kv_loads = [
        pltpu.make_async_copy(kf, kv_in.at[:, pl.ds(0, KW)], kv_in_sem.at[0]),
        pltpu.make_async_copy(vf, kv_in.at[:, pl.ds(KW, KW)], kv_in_sem.at[1]),
    ]
    q_loads = [
        pltpu.make_async_copy(qf.at[:, pl.ds(c * CHUNK, CHUNK)], q_in.at[c], in_sem.at[c])
        for c in range(CHUNKS)
    ]
    for load in kv_loads + q_loads:
        load.start()

    count = count_ref[0]
    counts[me] = jnp.full(counts.shape[1:], count, jnp.int32)

    for slot in range(LAST):
        @pl.when(me < LAST - slot)
        def _():
            window[slot] = jnp.zeros(window.shape[1:], BF16)

    @pl.when(me == 0)
    def _():
        kv_got[...] = jnp.zeros_like(kv_got)
        q_got[...] = jnp.zeros_like(q_got)

    barrier = pltpu.get_barrier_semaphore()

    @pl.loop(1, n)
    def _(step):
        pl.semaphore_signal(barrier, inc=1, device_id={"seq": lax.rem(me + step, n)})

    pl.semaphore_wait(barrier, n - 1)

    def remote(src, dst, send, recv, target):
        return pltpu.make_async_remote_copy(
            src_ref=src, dst_ref=dst, send_sem=send, recv_sem=recv, device_id={"seq": target}
        )

    def count_copy(sender, target):
        return remote(counts.at[sender], counts.at[sender], cnt_send.at[target], cnt_recv.at[sender], target)

    @pl.loop(me + 1, n)
    def _(target):
        count_copy(me, target).start()

    for load in kv_loads:
        load.wait()
    ending = one_hot(SPAN, cap, count - SPAN)
    kv_tail[...] = jnp.dot(ending, kv_in[...], preferred_element_type=F32).astype(BF16)

    def tail_of(c):
        q_loads[c].wait()
        q_tail[c] = jnp.dot(ending, q_in[c], preferred_element_type=F32).astype(BF16)

    tail_copy = remote(kv_tail, kv_got, tail_send, tail_recv, me + 1)

    def q_copy(c):
        return remote(q_tail.at[c], q_got.at[c], q_send.at[c], q_recv.at[c], me + 1)

    tail_of(0)

    @pl.when(me < n - 1)
    def _():
        tail_copy.start()

    for c in range(1, EARLY + 1):
        tail_of(c)

        @pl.when(me < n - 1)
        def _(c=c):
            q_copy(c - 1).start()

    for c in range(EARLY + 1, CHUNKS):
        tail_of(c)

    row = lax.broadcasted_iota(jnp.int32, (SPAN, SPAN), 0)
    column = lax.broadcasted_iota(jnp.int32, (SPAN, SPAN), 1)
    own_clip = seg_ref[pl.ds(me, 1), :]
    clip_column = jnp.sum(jnp.where(row == column, own_clip, 0), axis=1, keepdims=True)
    lane = lax.broadcasted_iota(jnp.int32, (SPAN, HEAD_DIM), 1)
    clips[...] = jnp.where(lane == clip_column, 1.0, 0.0).astype(BF16)
    causal[...] = jnp.where(column <= row, 0.0, LOW)
    clip_row = lax.broadcasted_iota(jnp.int32, (HEAD_DIM, SPAN), 0)
    for slot in range(WINDOW):
        block = me - LAST + slot
        key_clip = seg_ref[pl.ds(jnp.maximum(block, 0), 1), :]
        outside = jnp.where((key_clip == clip_row) & (block >= 0), 0.0, LOW).astype(BF16)
        for g in range(KV_HEADS):
            keys_t[g, HEAD_DIM:, slot * SPAN:(slot + 1) * SPAN] = outside

    @pl.loop(0, me)
    def _(sender):
        count_copy(sender, me).wait_recv()

    device = lax.broadcasted_iota(jnp.int32, counts.shape, 0)
    before = jnp.sum(jnp.where(device < me, counts[...], 0), axis=0)
    lead_in = before[0:1, 0:1] - me * SPAN
    start_row = lax.broadcasted_iota(jnp.int32, (SPAN, 2 * SPAN), 0)
    start_column = lax.broadcasted_iota(jnp.int32, (SPAN, 2 * SPAN), 1)
    shift = jnp.where(start_column + lead_in == start_row + SPAN, 1.0, 0.0).astype(BF16)

    @pl.when(me > 0)
    def _():
        tail_copy.wait_recv()

    def placed(arrived, own):
        both = jnp.concatenate([arrived, own], axis=0)
        return jnp.dot(shift, both, preferred_element_type=F32).astype(BF16)

    window[LAST] = placed(kv_got[...], kv_in[:SPAN])

    def lay_out(slot):
        for g in range(KV_HEADS):
            keys_t[g, :HEAD_DIM, slot * SPAN:(slot + 1) * SPAN] = window[
                slot, :, g * HEAD_DIM:(g + 1) * HEAD_DIM
            ].T
            vals[g, slot * SPAN:(slot + 1) * SPAN, :] = window[
                slot, :, KW + g * HEAD_DIM:KW + (g + 1) * HEAD_DIM
            ]

    lay_out(LAST)

    def block_copy(src, dst, target):
        return remote(window.at[src], window.at[dst], kv_send.at[dst], kv_recv.at[dst], target)

    near = block_copy(LAST, 2, me + 2)
    far = block_copy(LAST, 0, me + 4)
    partner = me + 1 - 2 * core
    beside = (block_copy(LAST, 3, partner), block_copy(2, 3, partner))
    across = (block_copy(2, 1, partner), block_copy(0, 1, partner))

    @pl.when(core == 0)
    def _():
        beside[0].start()

    @pl.when(me + 2 < n)
    def _():
        near.start()

    @pl.when(me + 4 < n)
    def _():
        far.start()

    @pl.when(me < n - 1)
    def _():
        for c in range(EARLY, CHUNKS):
            q_copy(c).start()

    @pl.when(me >= 2)
    def _():
        near.wait_recv()

        @pl.when(core == 0)
        def _():
            across[0].start()

        @pl.when(core == 1)
        def _():
            beside[1].start()

    lay_out(2)

    @pl.when(me >= 4)
    def _():
        far.wait_recv()

        @pl.when(core == 1)
        def _():
            across[1].start()

    lay_out(0)

    @pl.when(me >= 1)
    def _():
        beside[0].wait_recv()

    lay_out(3)

    @pl.when(me >= 3)
    def _():
        across[0].wait_recv()

    lay_out(1)

    scale = math.log2(math.e) / math.sqrt(HEAD_DIM)
    chunks_per_group = CHUNKS // KV_HEADS

    def out_copy(c):
        return pltpu.make_async_copy(
            o_buf.at[c], out.at[:, pl.ds(pl.multiple_of(c * CHUNK, CHUNK), CHUNK)], out_sem.at[c]
        )

    @pl.loop(0, CHUNKS)
    def _(c):
        @pl.when(me > 0)
        def _():
            q_copy(c).wait_recv()

        queries = placed(q_got[c], q_in[c, :SPAN])
        g = c // chunks_per_group
        for h in range(CHUNK_HEADS):
            query = jnp.concatenate([queries[:, h * HEAD_DIM:(h + 1) * HEAD_DIM], clips[...]], axis=1)
            scores = jnp.dot(query, keys_t[g], preferred_element_type=F32)
            past, own = scores[:, :LAST * SPAN], scores[:, LAST * SPAN:] + causal[...]
            peak = jnp.maximum(
                jnp.max(past, axis=1, keepdims=True), jnp.max(own, axis=1, keepdims=True)
            )
            weights = jnp.exp2((jnp.concatenate([past, own], axis=1) - peak) * scale)
            total = jnp.sum(weights, axis=1, keepdims=True)
            summed = jnp.dot(weights.astype(BF16), vals[g], preferred_element_type=F32)
            o_buf[c, :, h * HEAD_DIM:(h + 1) * HEAD_DIM] = (summed / total).astype(BF16)
        out_copy(c).start()

    @pl.loop(0, CHUNKS)
    def _(c):
        out_copy(c).wait()

    @pl.when(me < n - 1)
    def _():
        tail_copy.wait_send()
        for c in range(CHUNKS):
            q_copy(c).wait_send()

    @pl.when(me + 2 < n)
    def _():
        near.wait_send()

    @pl.when(me + 4 < n)
    def _():
        far.wait_send()

    @pl.when(core == 0)
    def _():
        beside[0].wait_send()

        @pl.when(me >= 2)
        def _():
            across[0].wait_send()

    @pl.when(core == 1)
    def _():
        @pl.when(me >= 2)
        def _():
            beside[1].wait_send()

        @pl.when(me >= 4)
        def _():
            across[1].wait_send()

    @pl.loop(me + 1, n)
    def _(target):
        count_copy(me, target).wait_send()


def shards(n, query_frames, key_frames, value_frames, token_counts, segments):
    cap = query_frames.shape[0]
    dma = pltpu.SemaphoreType.DMA
    vmem = pltpu.VMEM
    return pl.pallas_call(
        functools.partial(kernel, n),
        out_shape=jax.ShapeDtypeStruct((SPAN, Q_HEADS * HEAD_DIM), BF16),
        in_specs=[
            pl.BlockSpec(memory_space=pltpu.SMEM),
            pl.BlockSpec(memory_space=pltpu.VMEM),
            pl.BlockSpec(memory_space=pl.ANY),
            pl.BlockSpec(memory_space=pl.ANY),
            pl.BlockSpec(memory_space=pl.ANY),
        ],
        out_specs=pl.BlockSpec(memory_space=pl.ANY),
        scratch_shapes=[
            vmem((n, 8, 128), jnp.int32),
            vmem((CHUNKS, cap, CHUNK), BF16),
            vmem((CHUNKS, SPAN, CHUNK), BF16),
            vmem((CHUNKS, SPAN, CHUNK), BF16),
            vmem((cap, 2 * KW), BF16),
            vmem((SPAN, 2 * KW), BF16),
            vmem((SPAN, 2 * KW), BF16),
            vmem((WINDOW, SPAN, 2 * KW), BF16),
            vmem((KV_HEADS, 2 * HEAD_DIM, WINDOW * SPAN), BF16),
            vmem((KV_HEADS, WINDOW * SPAN, HEAD_DIM), BF16),
            vmem((SPAN, SPAN), F32),
            vmem((SPAN, HEAD_DIM), BF16),
            vmem((CHUNKS, SPAN, CHUNK), BF16),
            dma((CHUNKS,)),
            dma((2,)),
            dma((CHUNKS,)),
            dma((n,)),
            dma((n,)),
            dma,
            dma,
            dma((CHUNKS,)),
            dma((CHUNKS,)),
            dma((WINDOW,)),
            dma((WINDOW,)),
        ],
        compiler_params=pltpu.CompilerParams(collective_id=0, has_side_effects=True),
    )(token_counts, segments.reshape(-1, SPAN), query_frames, key_frames, value_frames)


def solution(mesh):
    in_specs = (
        P(("group", "seq"), None),
        P(("group", "seq"), None),
        P(("group", "seq"), None),
        P(("group", "seq")),
        P("group"),
    )
    out_specs = P(("group", "seq"), None)
    return jax.shard_map(
        functools.partial(shards, mesh.shape["seq"]),
        mesh=mesh, in_specs=in_specs, out_specs=out_specs, check_vma=False,
    )
```

time: 150 us -> 70.4 us (0.47)
  the two profiles are of different devices: /device:TPU:0 before, /device:TPU:10 now
where the time goes in v1:
time: 70.4 us; the launch traced here: 70.1 us
  Pallas kernels  64.9 us (92%)
  local copies, waits for them, and re-layouts  4.46 us (6%)
    pallas_call x1, Pallas kernels, shards(): pl.pallas_call(functools.partial(kernel, n), out_shape=jax.ShapeDtypeStru...  64.9 us
    unnamed x1, local copies, waits for them, and re-layouts  3.13 us

profile of v1, /device:TPU:10, one launch (start us, length us, event | category | flops | bytes accessed | tf_op | source)
XLA Modules:
  0.0 70.1 jit_solution(1700503042579014742)
XLA Ops:
  0.7 1.3 %reshape.3.seg_ref = s32[16,256]{1,0:T(8,128)} reshape(s32[4096]{0:T(1024)} %param.9) | data formatting | bytes 32768 | tf_op jit(solution)/shard_map/reshape | solution.py:337
  2.0 64.9 %shard_map.55 = bf16[256,4096]{1,0:T(8,128)(2,1)} custom-call(s32[1]{0:T(128)S(6)} %copy.7.count_ref, s32[16,256]{1,0:T(8,128)} %reshape.3.seg_ref, bf16[512,4096]{1,0:T(8,128)(2,1)} %qf.1, bf16[512,512]{1,0:T(8,128)(2,1)} %kf.1, bf16[512,512]{1,0:T(8,128)(2,1)} %vf.1), custom_call_target="tpu_custom_call" | custom-call | tf_op jit(solution)/shard_map/pallas_call | solution.py:299
  66.9 3.1 %copy.8 = bf16[256,4096]{1,0:T(8,128)(2,1)} copy(bf16[256,4096]{1,0:T(8,128)(2,1)} %shard_map.55) | data formatting | bytes 4194304

commit v2 on v1

--- a/solution.py
+++ b/solution.py
@@ -16,7 +16,8 @@
 CHUNK_HEADS = 4
 CHUNK = CHUNK_HEADS * HEAD_DIM
 CHUNKS = Q_HEADS // CHUNK_HEADS
-EARLY = 2
+HALF = SPAN // 2
+WIDE = WINDOW * SPAN - HALF
 KW = KV_HEADS * HEAD_DIM
 LAST = WINDOW - 1
 LOW = -(2.0**100)
@@ -32,7 +33,7 @@
 
 def kernel(
     n, count_ref, seg_ref, qf, kf, vf, out,
-    counts, q_in, q_tail, q_got, kv_in, kv_tail, kv_got, window, keys_t, vals, causal, clips, o_buf,
+    counts, q_in, q_tail, q_got, kv_in, kv_tail, kv_got, window, keys_t, vals, clips, o_buf,
     in_sem, kv_in_sem, out_sem, cnt_send, cnt_recv, tail_send, tail_recv, q_send, q_recv, kv_send, kv_recv,
 ):
     me = lax.axis_index("seq")
@@ -97,36 +98,28 @@
     def q_copy(c):
         return remote(q_tail.at[c], q_got.at[c], q_send.at[c], q_recv.at[c], me + 1)
 
-    tail_of(0)
-
-    @pl.when(me < n - 1)
-    def _():
-        tail_copy.start()
-
-    for c in range(1, EARLY + 1):
-        tail_of(c)
-
-        @pl.when(me < n - 1)
-        def _(c=c):
-            q_copy(c - 1).start()
-
-    for c in range(EARLY + 1, CHUNKS):
-        tail_of(c)
+    def clip_row_of(block):
+        first = pl.multiple_of(block * SPAN, SPAN)
+        return seg_ref[pl.ds(first, SPAN)].reshape(1, SPAN)
 
     row = lax.broadcasted_iota(jnp.int32, (SPAN, SPAN), 0)
     column = lax.broadcasted_iota(jnp.int32, (SPAN, SPAN), 1)
-    own_clip = seg_ref[pl.ds(me, 1), :]
+    own_clip = clip_row_of(me)
     clip_column = jnp.sum(jnp.where(row == column, own_clip, 0), axis=1, keepdims=True)
     lane = lax.broadcasted_iota(jnp.int32, (SPAN, HEAD_DIM), 1)
     clips[...] = jnp.where(lane == clip_column, 1.0, 0.0).astype(BF16)
-    causal[...] = jnp.where(column <= row, 0.0, LOW)
     clip_row = lax.broadcasted_iota(jnp.int32, (HEAD_DIM, SPAN), 0)
     for slot in range(WINDOW):
         block = me - LAST + slot
-        key_clip = seg_ref[pl.ds(jnp.maximum(block, 0), 1), :]
+        key_clip = clip_row_of(jnp.maximum(block, 0))
         outside = jnp.where((key_clip == clip_row) & (block >= 0), 0.0, LOW).astype(BF16)
         for g in range(KV_HEADS):
             keys_t[g, HEAD_DIM:, slot * SPAN:(slot + 1) * SPAN] = outside
+    vals[:, :, HEAD_DIM:] = jnp.ones((KV_HEADS, WINDOW * SPAN, HEAD_DIM), BF16)
+
+    @pl.when(me < n - 1)
+    def _():
+        tail_copy.start()
 
     @pl.loop(0, me)
     def _(sender):
@@ -154,7 +147,7 @@
             keys_t[g, :HEAD_DIM, slot * SPAN:(slot + 1) * SPAN] = window[
                 slot, :, g * HEAD_DIM:(g + 1) * HEAD_DIM
             ].T
-            vals[g, slot * SPAN:(slot + 1) * SPAN, :] = window[
+            vals[g, slot * SPAN:(slot + 1) * SPAN, :HEAD_DIM] = window[
                 slot, :, KW + g * HEAD_DIM:KW + (g + 1) * HEAD_DIM
             ]
 
@@ -181,10 +174,16 @@
     def _():
         far.start()
 
+    for c in range(CHUNKS):
+        tail_of(c)
+        if c > 0:
+            @pl.when(me < n - 1)
+            def _(c=c):
+                q_copy(c - 1).start()
+
     @pl.when(me < n - 1)
     def _():
-        for c in range(EARLY, CHUNKS):
-            q_copy(c).start()
+        q_copy(CHUNKS - 1).start()
 
     @pl.when(me >= 2)
     def _():
@@ -224,6 +223,9 @@
 
     scale = math.log2(math.e) / math.sqrt(HEAD_DIM)
     chunks_per_group = CHUNKS // KV_HEADS
+    half_row = lax.broadcasted_iota(jnp.int32, (HALF, HALF), 0)
+    half_column = lax.broadcasted_iota(jnp.int32, (HALF, HALF), 1)
+    lower = half_column <= half_row
 
     def out_copy(c):
         return pltpu.make_async_copy(
@@ -239,16 +241,28 @@
         queries = placed(q_got[c], q_in[c, :SPAN])
         g = c // chunks_per_group
         for h in range(CHUNK_HEADS):
-            query = jnp.concatenate([queries[:, h * HEAD_DIM:(h + 1) * HEAD_DIM], clips[...]], axis=1)
-            scores = jnp.dot(query, keys_t[g], preferred_element_type=F32)
-            past, own = scores[:, :LAST * SPAN], scores[:, LAST * SPAN:] + causal[...]
-            peak = jnp.maximum(
-                jnp.max(past, axis=1, keepdims=True), jnp.max(own, axis=1, keepdims=True)
-            )
-            weights = jnp.exp2((jnp.concatenate([past, own], axis=1) - peak) * scale)
-            total = jnp.sum(weights, axis=1, keepdims=True)
-            summed = jnp.dot(weights.astype(BF16), vals[g], preferred_element_type=F32)
-            o_buf[c, :, h * HEAD_DIM:(h + 1) * HEAD_DIM] = (summed / total).astype(BF16)
+            columns = slice(h * HEAD_DIM, (h + 1) * HEAD_DIM)
+            for part in range(2):
+                rows = slice(part * HALF, (part + 1) * HALF)
+                reach = slice(part * HALF, part * HALF + WIDE)
+                query = jnp.concatenate([queries[rows, columns], clips[rows]], axis=1)
+                scores = jnp.dot(query, keys_t[g, :, reach], preferred_element_type=F32)
+                ends = jnp.where(lower, scores[:, WIDE - HALF:], scores[:, :HALF])
+                middle = scores[:, HALF:WIDE - HALF]
+                peak = jnp.maximum(
+                    jnp.max(ends, axis=1, keepdims=True), jnp.max(middle, axis=1, keepdims=True)
+                )
+                end_weights = jnp.exp2((ends - peak) * scale)
+                weights = jnp.concatenate(
+                    [
+                        jnp.where(lower, 0.0, end_weights).astype(BF16),
+                        jnp.exp2((middle - peak) * scale).astype(BF16),
+                        jnp.where(lower, end_weights, 0.0).astype(BF16),
+                    ],
+                    axis=1,
+                )
+                summed = jnp.dot(weights, vals[g, reach, :], preferred_element_type=F32)
+                o_buf[c, rows, columns] = (summed[:, :HEAD_DIM] / summed[:, HEAD_DIM:]).astype(BF16)
         out_copy(c).start()
 
     @pl.loop(0, CHUNKS)
@@ -317,8 +331,7 @@
             vmem((SPAN, 2 * KW), BF16),
             vmem((WINDOW, SPAN, 2 * KW), BF16),
             vmem((KV_HEADS, 2 * HEAD_DIM, WINDOW * SPAN), BF16),
-            vmem((KV_HEADS, WINDOW * SPAN, HEAD_DIM), BF16),
-            vmem((SPAN, SPAN), F32),
+            vmem((KV_HEADS, WINDOW * SPAN, 2 * HEAD_DIM), BF16),
             vmem((SPAN, HEAD_DIM), BF16),
             vmem((CHUNKS, SPAN, CHUNK), BF16),
             dma((CHUNKS,)),
@@ -334,7 +347,7 @@
             dma((WINDOW,)),
         ],
         compiler_params=pltpu.CompilerParams(collective_id=0, has_side_effects=True),
-    )(token_counts, segments.reshape(-1, SPAN), query_frames, key_frames, value_frames)
+    )(token_counts, segments, query_frames, key_frames, value_frames)
 
 
 def solution(mesh):

time: 70.4 us -> 66.1 us (0.939)
  Pallas kernels: 64.9 us -> 61.7 us
  local copies, waits for them, and re-layouts: 4.46 us -> 3.13 us
    pallas_call x1, Pallas kernels: 64.9 us -> 61.7 us  [shards(): pl.pallas_call(functools.partial(kernel, n), out_shape=jax.ShapeDtypeStru...]
    reshape x1 -> x0, local copies, waits for them, and re-layouts: 1.33 us -> none  [shards(): segments.reshape(-1, SPAN)]
where the time goes in v2:
time: 66.1 us; the launch traced here: 65.5 us
  Pallas kernels  61.7 us (93%)
  local copies, waits for them, and re-layouts  3.13 us (5%)
    pallas_call x1, Pallas kernels, shards(): pl.pallas_call(functools.partial(kernel, n), out_shape=jax.ShapeDtypeStru...  61.7 us
    unnamed x1, local copies, waits for them, and re-layouts  3.13 us

profile of v2, /device:TPU:10, one launch (start us, length us, event | category | flops | bytes accessed | tf_op | source)
XLA Modules:
  0.0 65.5 jit_solution(15257744932209604695)
XLA Ops:
  0.7 61.7 %shard_map.55 = bf16[256,4096]{1,0:T(8,128)(2,1)} custom-call(s32[1]{0:T(128)S(6)} %copy.7.count_ref, s32[4096]{0:T(1024)} %seg_ref.1, bf16[512,4096]{1,0:T(8,128)(2,1)} %qf.1, bf16[512,512]{1,0:T(8,128)(2,1)} %kf.1, bf16[512,512]{1,0:T(8,128)(2,1)} %vf.1), custom_call_target="tpu_custom_call" | custom-call | tf_op jit(solution)/shard_map/pallas_call | solution.py:313
  62.3 3.1 %copy.8 = bf16[256,4096]{1,0:T(8,128)(2,1)} copy(bf16[256,4096]{1,0:T(8,128)(2,1)} %shard_map.55) | data formatting | bytes 4194304
